TPU v7x, 32 devices: a whole 2x2x4 slice. The times are simulated.
32 devices in a mesh: srv: 16 (over z, y, x), grp: 2 (over core).
Axes of the slice: x: 2, y: 2, z: 4, core: 2. Of those that a mesh axis runs over, the one named last changes fastest.
Arguments:
- basis_modes: float32 [64, 64, 3072], P(None, ('srv', 'grp')), may hold values from -10 to 10
- weights: float32 [64], replicated, may hold values from 0.5 to 4
- snapshots: float32 [16, 64, 3072], P(None, 'srv', 'grp'), may hold values from -10 to 10
Outputs:
- new_modes: float32 [80, 64, 3072], P(None, ('srv', 'grp'))
- factor: float32 [80, 80], replicated
All inputs are finite; a program needn't handle non-finite values.
Results may differ from a plain program's by a relative error of at most 0.00009.
Values sent between devices are 32-bit elements; how exact they have to be, the bound alone decides.
No kernel may reach another device: no remote copies, remote signals or barrier semaphores. Data moves between devices by JAX's collectives and lax.ppermute only.
A program may use at most 64 MiB of HBM per device.

v0:
```python
import jax
import jax.numpy as jnp
from jax import lax
from jax.sharding import PartitionSpec as P

MODES = 64
SNAPS = 16


def merged_factor(local_gram):
    return jnp.linalg.cholesky(lax.psum(local_gram, ("srv", "grp")))


def per_device(basis_modes, weights, snapshots):
    width = MODES + SNAPS
    total_cells = (
        basis_modes.shape[1] * basis_modes.shape[2] * lax.axis_size("srv") * lax.axis_size("grp")
    )
    scaled = basis_modes * weights[:, None, None]
    arrived = lax.all_to_all(snapshots, "grp", split_axis=1, concat_axis=2, tiled=True)
    panel = jnp.concatenate([scaled, arrived], axis=0).reshape(width, -1)
    local_gram = (
        jnp.dot(panel, panel.T, precision=lax.Precision.HIGHEST, preferred_element_type=jnp.float32)
        / total_cells
    )
    factor = merged_factor(local_gram)
    inverse = lax.linalg.triangular_solve(
        factor, jnp.eye(width, dtype=jnp.float32), left_side=True, lower=True
    )
    result = jnp.dot(
        inverse, panel, precision=lax.Precision.HIGHEST, preferred_element_type=jnp.float32
    )
    result = result.reshape(width, basis_modes.shape[1], basis_modes.shape[2])
    return (result, factor)


def solution(mesh):
    in_specs = (P(None, ("srv", "grp"), None), P(), P(None, "srv", "grp"))
    out_specs = (P(None, ("srv", "grp"), None), P())
    return jax.shard_map(
        per_device, mesh=mesh, in_specs=in_specs, out_specs=out_specs, check_vma=False
    )
```

profile of v0, /device:TPU:0, one launch (start us, length us, event | category | flops | bytes accessed | tf_op | source)
XLA Modules:
  0.0 77.2 jit_solution(11390154502908591722)
XLA Ops:
  0.6 0.0 copy-start
  0.6 0.0 copy-start.1
  0.6 1.2 %copy.19 = f32[16,4,1536]{2,0,1:T(8,128)S(1)} copy(f32[16,4,1536]{2,1,0:T(4,128)} %param.5) | data formatting | bytes 786432 | tf_op args[2]
  1.9 4.0 %all_to_all.18 = f32[16,4,1536]{2,0,1:T(8,128)S(1)} all-to-all(f32[16,4,1536]{2,0,1:T(8,128)S(1)} %copy.19), channel_id=1, replica_groups=mesh['srv'=16,'grp'=2] {'grp'}, dimensions={1} | all-to-all | bytes 786432 | tf_op jit(solution)/shard_map/all_to_all | solution.py:20
  5.9 1.1 %copy.41 = f32[16,2,2,1536]{3,1,0,2:T(2,128)} copy(f32[16,2,2,1536]{3,0,2,1:T(8,128)S(1)} %bitcast.35) | data formatting | bytes 786432 | tf_op jit(solution)/shard_map/all_to_all | solution.py:20
  7.0 0.3 copy.42
  7.3 0.0 copy-done
  7.3 0.0 copy-done.1
  7.3 0.5 copy_multiply_fusion
  7.8 0.5 fusion.17
  8.4 2.1 %all_to_all.16 = f32[16,2,3072]{2,0,1:T(8,128)} reshape(f32[16,2,2,1536]{3,2,0,1:T(2,128)} %bitcast.38) | data formatting | bytes 786432 | tf_op jit(solution)/shard_map/all_to_all | solution.py:20
  10.4 3.4 %fusion.10 = f32[80,80]{0,1:T(8,128)} fusion(f32[16,2,3072]{2,0,1:T(8,128)} %all_to_all.16, f32[64,2,3072]{2,0,1:T(8,128)S(1)} %copy_multiply_fusion), kind=kOutput, calls=%fused_computation.11 | convolution fusion | flops 472357120 | bytes 1991680 | tf_op jit(solution)/shard_map/dot_general | solution.py:23
  13.9 42.4 %psum.7 = f32[80,80]{0,1:T(8,128)S(1)} all-reduce(f32[80,80]{0,1:T(8,128)} %fusion.10), channel_id=1, replica_groups=mesh['srv'=16,'grp'=2] {'srv','grp'}, use_global_device_ids=true, to_apply=%region_0.0 | all-reduce | flops 6400 | bytes 51200 | tf_op jit(solution)/shard_map/psum | solution.py:11
  56.2 0.1 copy.23
  56.3 7.3 %cholesky.17 = f32[80,80]{1,0:T(8,128)S(1)} custom-call(f32[80,80]{1,0:T(8,128)S(1)} %fusion.14), custom_call_target="Cholesky" | custom-call | tf_op jit(solution)/shard_map/jit(cholesky)/cholesky | solution.py:11
  63.7 0.6 compare_reduce_fusion
  64.3 1.3 %select_bitcast_fusion = (f32[1,80,80]{2,1,0:T(8,128)S(1)}, f32[80,80]{1,0:T(8,128)}) fusion(f32[80,80]{1,0:T(8,128)S(1)} %cholesky.17, pred[]{:T(512)} %compare_reduce_fusion), kind=kLoop, calls=%fused_computation.17 | loop fusion | flops 25600 | bytes 76801 | tf_op jit(solution)/shard_map/triangular_solve | solution.py:27
  65.6 6.1 %custom-call.6 = f32[1,80,80]{1,2,0:T(8,128)S(1)} custom-call(f32[1,80,80]{2,1,0:T(8,128)S(1)} %get-tuple-element.8), custom_call_target="InvertDiagBlocksLowerTriangular" | custom-call | tf_op jit(solution)/shard_map/triangular_solve | solution.py:27
  71.7 0.2 convolution_bitcast_fusion
  72.0 0.3 concatenate.12
  72.3 0.1 copy.31
  72.4 0.1 pad_maximum_fusion
  72.6 1.8 %fusion = f32[80,2,3072]{2,0,1:T(8,128)S(1)} fusion(f32[80,80,1]{1,0,2:T(8,128)S(1)} %convolution_bitcast_fusion, f32[10,2,8,3072]{3,2,1,0:T(8,128)S(1)} %bitcast.33), kind=kOutput, calls=%fused_computation | convolution fusion | flops 471859200 | bytes 3957760 | tf_op jit(solution)/shard_map/dot_general | solution.py:30
  74.4 2.8 %copy.26 = f32[80,2,3072]{2,1,0:T(2,128)} copy(f32[80,2,3072]{2,0,1:T(8,128)S(1)} %fusion) | data formatting | bytes 3932160
  (2 shorter events, 0.0 us)
Async XLA Ops:
  0.6 6.7 %copy-start = (f32[64,2,3072]{2,1,0:T(2,128)S(1)}, f32[64,2,3072]{2,1,0:T(2,128)}, u32[]{:S(2)}) copy-start(f32[64,2,3072]{2,1,0:T(2,128)} %param.3) | copy-start | bytes 4718596
  0.6 6.7 %copy-start.1 = (f32[64]{0:T(128)S(1)}, f32[64]{0:T(128)}, u32[]{:S(2)}) copy-start(f32[64]{0:T(128)} %param.4) | copy-start | bytes 772
where the time goes:
time: 77.6 us; the launch traced here: 77.2 us
  blocking collectives  46.4 us (60%)
  other arithmetic  16.6 us (21%)
  local copies, waits for them, and re-layouts  7.98 us (10%)
  matrix products  5.45 us (7%)
    psum x1, blocking collectives, merged_factor(): return jnp.linalg.cholesky(lax.psum(local_gram, ('srv', 'grp')))  42.4 us
    another operation x3, other arithmetic, merged_factor(): return jnp.linalg.cholesky(lax.psum(local_gram, ('srv', 'grp')))  7.98 us
    another operation x2, other arithmetic, per_device(): lax.linalg.triangular_solve(factor, jnp.eye(width, dtype=jnp.float32), le...  7.4 us
    all_to_all x1, blocking collectives, per_device(): lax.all_to_all(snapshots, 'grp', split_axis=1, concat_axis=2, tiled=True)  4.05 us
    unnamed x6, local copies, waits for them, and re-layouts  4.04 us
    all_to_all x3, local copies, waits for them, and re-layouts, per_device(): lax.all_to_all(snapshots, 'grp', split_axis=1, concat_axis=2, tiled=True)  3.43 us
    dot_general x1, matrix products, per_device(): jnp.dot(panel, panel.T, precision=lax.Precision.HIGHEST, preferred_elemen...  3.41 us
    dot_general x1, matrix products, per_device(): jnp.dot(inverse, panel, precision=lax.Precision.HIGHEST, preferred_elemen...  1.82 us

commit v1 on v0

--- a/solution.py
+++ b/solution.py
@@ -8,7 +8,7 @@
 
 
 def merged_factor(local_gram):
-    return jnp.linalg.cholesky(lax.psum(local_gram, ("srv", "grp")))
+    return jnp.linalg.cholesky(lax.psum(lax.psum(local_gram, "grp"), "srv"))
 
 
 def per_device(basis_modes, weights, snapshots):

time: 77.6 us -> 118 us (1.52)
  blocking collectives: 46.4 us -> 86.8 us
    psum x1 -> x2, blocking collectives: 42.4 us -> 82.7 us  [merged_factor(): return jnp.linalg.cholesky(lax.psum(lax.psum(local_gram, 'grp'), 'srv'))]
where the time goes in v1:
time: 118 us
  blocking collectives  86.8 us (74%)
  other arithmetic  16.6 us (14%)
  local copies, waits for them, and re-layouts  7.99 us (7%)
  matrix products  5.45 us (5%)
    psum x2, blocking collectives, merged_factor(): return jnp.linalg.cholesky(lax.psum(lax.psum(local_gram, 'grp'), 'srv'))  82.7 us
    another operation x3, other arithmetic, merged_factor(): return jnp.linalg.cholesky(lax.psum(lax.psum(local_gram, 'grp'), 'srv'))  7.98 us
    another operation x2, other arithmetic, per_device(): lax.linalg.triangular_solve(factor, jnp.eye(width, dtype=jnp.float32), le...  7.4 us
    all_to_all x1, blocking collectives, per_device(): lax.all_to_all(snapshots, 'grp', split_axis=1, concat_axis=2, tiled=True)  4.05 us
    unnamed x6, local copies, waits for them, and re-layouts  4.04 us
    all_to_all x3, local copies, waits for them, and re-layouts, per_device(): lax.all_to_all(snapshots, 'grp', split_axis=1, concat_axis=2, tiled=True)  3.43 us
    dot_general x1, matrix products, per_device(): jnp.dot(panel, panel.T, precision=lax.Precision.HIGHEST, preferred_elemen...  3.41 us

profile of v1, /device:TPU:0, one launch (start us, length us, event | category | flops | bytes accessed | tf_op | source)
XLA Modules:
  0.0 117.5 jit_solution(3051410211175186194)
XLA Ops:
  0.6 0.0 copy-start
  0.6 0.0 copy-start.1
  0.6 1.2 %copy.19 = f32[16,4,1536]{2,0,1:T(8,128)S(1)} copy(f32[16,4,1536]{2,1,0:T(4,128)} %param.5) | data formatting | bytes 786432 | tf_op args[2]
  1.9 4.0 %all_to_all.18 = f32[16,4,1536]{2,0,1:T(8,128)S(1)} all-to-all(f32[16,4,1536]{2,0,1:T(8,128)S(1)} %copy.19), channel_id=1, replica_groups=mesh['srv'=16,'grp'=2] {'grp'}, dimensions={1} | all-to-all | bytes 786432 | tf_op jit(solution)/shard_map/all_to_all | solution.py:20
  5.9 1.1 copy.41
  7.0 0.3 copy.42
  7.3 0.0 copy-done
  7.3 0.0 copy-done.1
  7.3 0.5 copy_multiply_fusion
  7.8 0.5 fusion.17
  8.4 2.1 %all_to_all.16 = f32[16,2,3072]{2,0,1:T(8,128)} reshape(f32[16,2,2,1536]{3,2,0,1:T(2,128)} %bitcast.38) | data formatting | bytes 786432 | tf_op jit(solution)/shard_map/all_to_all | solution.py:20
  10.4 3.4 %fusion.10 = f32[80,80]{0,1:T(8,128)} fusion(f32[16,2,3072]{2,0,1:T(8,128)} %all_to_all.16, f32[64,2,3072]{2,0,1:T(8,128)S(1)} %copy_multiply_fusion), kind=kOutput, calls=%fused_computation.11 | convolution fusion | flops 472357120 | bytes 1991680 | tf_op jit(solution)/shard_map/dot_general | solution.py:23
  13.9 4.1 %psum.14 = f32[80,80]{0,1:T(8,128)S(1)} all-reduce(f32[80,80]{0,1:T(8,128)} %fusion.10), channel_id=1, replica_groups=mesh['srv'=16,'grp'=2] {'grp'}, use_global_device_ids=true, to_apply=%region_0.0 | all-reduce | flops 6400 | bytes 51200 | tf_op jit(solution)/shard_map/psum | solution.py:11
  17.9 78.7 %psum.15 = f32[80,80]{0,1:T(8,128)S(1)} all-reduce(f32[80,80]{0,1:T(8,128)S(1)} %psum.14), channel_id=1, replica_groups=mesh['srv'=16,'grp'=2] {'srv'}, use_global_device_ids=true, to_apply=%region_1.0 | all-reduce | flops 6400 | bytes 51200 | tf_op jit(solution)/shard_map/psum | solution.py:11
  96.6 0.1 copy.23
  96.7 7.3 %cholesky.17 = f32[80,80]{1,0:T(8,128)S(1)} custom-call(f32[80,80]{1,0:T(8,128)S(1)} %fusion.14), custom_call_target="Cholesky" | custom-call | tf_op jit(solution)/shard_map/jit(cholesky)/cholesky | solution.py:11
  104.0 0.6 compare_reduce_fusion
  104.7 1.3 %select_bitcast_fusion = (f32[1,80,80]{2,1,0:T(8,128)S(1)}, f32[80,80]{1,0:T(8,128)}) fusion(f32[80,80]{1,0:T(8,128)S(1)} %cholesky.17, pred[]{:T(512)} %compare_reduce_fusion), kind=kLoop, calls=%fused_computation.17 | loop fusion | flops 25600 | bytes 76801 | tf_op jit(solution)/shard_map/triangular_solve | solution.py:27
  106.0 6.1 %custom-call.6 = f32[1,80,80]{1,2,0:T(8,128)S(1)} custom-call(f32[1,80,80]{2,1,0:T(8,128)S(1)} %get-tuple-element.8), custom_call_target="InvertDiagBlocksLowerTriangular" | custom-call | tf_op jit(solution)/shard_map/triangular_solve | solution.py:27
  112.1 0.2 convolution_bitcast_fusion
  112.3 0.3 concatenate.12
  112.7 0.1 copy.31
  112.8 0.1 pad_maximum_fusion
  112.9 1.8 %fusion = f32[80,2,3072]{2,0,1:T(8,128)S(1)} fusion(f32[80,80,1]{1,0,2:T(8,128)S(1)} %convolution_bitcast_fusion, f32[10,2,8,3072]{3,2,1,0:T(8,128)S(1)} %bitcast.33), kind=kOutput, calls=%fused_computation | convolution fusion | flops 471859200 | bytes 3957760 | tf_op jit(solution)/shard_map/dot_general | solution.py:30
  114.7 2.8 %copy.26 = f32[80,2,3072]{2,1,0:T(2,128)} copy(f32[80,2,3072]{2,0,1:T(8,128)S(1)} %fusion) | data formatting | bytes 3932160
  (2 shorter events, 0.0 us)
Async XLA Ops:
  0.6 6.7 %copy-start = (f32[64,2,3072]{2,1,0:T(2,128)S(1)}, f32[64,2,3072]{2,1,0:T(2,128)}, u32[]{:S(2)}) copy-start(f32[64,2,3072]{2,1,0:T(2,128)} %param.3) | copy-start | bytes 4718596
  0.6 6.7 %copy-start.1 = (f32[64]{0:T(128)S(1)}, f32[64]{0:T(128)}, u32[]{:S(2)}) copy-start(f32[64]{0:T(128)} %param.4) | copy-start | bytes 772
